TPU v7x, 32 devices: a 4x4x1 block of a 4x4x8 slice. The times are simulated.
32 devices in a mesh: stage: 1 (over z), fsdp: 4 (over y), tp: 8 (over x, core).
Axes of the slice: x: 4, y: 4, z: 1, core: 2. Of those that a mesh axis runs over, the one named last changes fastest.
The devices are a block of a 4x4x8 slice.
Arguments:
- weight: float32 [4, 1536, 12288], P('stage', 'fsdp', 'tp')
- momentum: float32 [4, 1536, 12288], P('stage', 'fsdp', 'tp')
- gradient: bfloat16 [4, 1536, 12288], P('stage', 'fsdp', 'tp')
- learn_rate: float32 [], replicated
- momentum_coef: float32 [], replicated
- weight_decay: float32 [], replicated
Outputs:
- output 1: float32 [4, 1536, 12288], P('stage', 'fsdp', 'tp')
- output 2: float32 [4, 1536, 12288], P('stage', 'fsdp', 'tp')
All inputs are finite; a program needn't handle non-finite values.
Results may differ from a plain program's by a relative error of at most 0.0156467.
Values are sent between devices in bfloat16 or wider.
A program may use at most 768 MiB of HBM per device.

v0:
```python
import math
import jax
import jax.numpy as jnp
from jax import lax
from jax.sharding import PartitionSpec as P

NS_STEPS = 5
COEF_A = 3.4445
COEF_B = -4.7750
COEF_C = 2.0315
EPSILON = 1e-7


def solution(mesh):
    block_spec = P('stage', 'fsdp', 'tp')
    scalar_spec = P()

    def muon_step(weight, momentum, gradient, learn_rate, momentum_coef, weight_decay):
        n_cols = weight.shape[2]

        def local_step(w_blk, m_blk, g_blk, rate_val, coef_val, decay_val):
            g_wide = g_blk.astype(jnp.float32)
            m_new = coef_val * m_blk + g_wide
            x_init = g_wide + coef_val * m_new
            sq_sum = lax.psum(jnp.sum(x_init * x_init, axis=(1, 2), keepdims=True), ('fsdp', 'tp'))
            x_cur = (x_init / (jnp.sqrt(sq_sum) + EPSILON)).astype(jnp.bfloat16)
            for _ in range(NS_STEPS):
                x_col = lax.all_gather(x_cur, 'fsdp', axis=1, tiled=True)
                gram_part = jnp.einsum('lrk,lsk->lrs', x_cur, x_col, preferred_element_type=jnp.float32)
                gram_blk = lax.psum_scatter(gram_part, 'tp', scatter_dimension=2, tiled=True).astype(jnp.bfloat16)
                gram_row = lax.all_gather(gram_blk, 'tp', axis=2, tiled=True)
                gram_col = lax.all_gather(gram_blk, 'fsdp', axis=1, tiled=True)
                gram_sq = jnp.einsum('lrk,lks->lrs', gram_row, gram_col, preferred_element_type=jnp.float32).astype(jnp.bfloat16)
                poly_blk = (COEF_B * gram_blk.astype(jnp.float32) + COEF_C * gram_sq.astype(jnp.float32)).astype(jnp.bfloat16)
                poly_row = lax.all_gather(poly_blk, 'tp', axis=2, tiled=True)
                poly_x = jnp.einsum('lrk,lkc->lrc', poly_row, x_col, preferred_element_type=jnp.float32)
                x_cur = (COEF_A * x_cur.astype(jnp.float32) + poly_x).astype(jnp.bfloat16)
            step_scale = rate_val * 0.2 * math.sqrt(n_cols)
            keep_scale = 1.0 - rate_val * decay_val
            w_new = keep_scale * w_blk - step_scale * x_cur.astype(jnp.float32)
            return w_new, m_new

        sharded = jax.shard_map(local_step, mesh=mesh, in_specs=(block_spec, block_spec, block_spec, scalar_spec, scalar_spec, scalar_spec), out_specs=(block_spec, block_spec), check_vma=False)
        return sharded(weight, momentum, gradient, learn_rate, momentum_coef, weight_decay)

    return muon_step
```

profile of v0, /device:TPU:97, one launch (start us, length us, event | category | flops | bytes accessed | tf_op | source)
XLA Modules:
  0.0 1892.8 jit_solution(10624188271278075483)
XLA Ops:
  18.9 49.7 %psum.7 = f32[4,1,1]{0,2,1:T(1,128)S(1)} all-reduce(f32[4,1,1]{0,2,1:T(1,128)S(1)} %bitcast.33), channel_id=1, replica_groups=mesh['stage'=1,'fsdp'=4,'tp'=8] {'fsdp','tp'}, use_global_device_ids=true, to_apply=%region_1.0 | all-reduce | flops 4 | bytes 32 | tf_op jit(solution)/shard_map/psum | solution.py:25
  77.8 167.7 %all-gather.21.cloned.1.call-done = bf16[4,1536,1536]{2,1,0:T(8,128)(2,1)} async-done(((bf16[4,384,1536]{2,1,0:T(8,128)(2,1)}), bf16[4,1536,1536]{2,1,0:T(8,128)(2,1)}) %all-gather.21.cloned.1.call-update) | async-done | bytes 18874384 | tf_op jit(solution)/shard_map/all_gather | solution.py:28
  263.0 55.1 %reduce-scatter.6.cloned.1.call-done = f32[4,384,192]{1,2,0:T(8,128)} async-done(((f32[4,384,1536]{1,2,0:T(8,128)}), f32[4,384,192]{1,2,0:T(8,128)}) %reduce-scatter.6.cloned.1.call-update) | async-done | bytes 1179664 | tf_op jit(solution)/shard_map/reduce_scatter | solution.py:30
  320.9 29.4 %all-gather.25.cloned.1.call-done = bf16[4,1536,192]{1,2,0:T(8,128)(2,1)} async-done(((bf16[4,384,192]{1,2,0:T(8,128)(2,1)}), bf16[4,1536,192]{1,2,0:T(8,128)(2,1)}) %all-gather.25.cloned.1.call-update) | async-done | bytes 2359312 | tf_op jit(solution)/shard_map/all_gather | solution.py:32
  350.4 34.2 %all-gather.23.cloned.1.call-done = bf16[4,384,1536]{1,2,0:T(8,128)(2,1)} async-done(((bf16[4,384,192]{1,2,0:T(8,128)(2,1)}), bf16[4,384,1536]{1,2,0:T(8,128)(2,1)}) %all-gather.23.cloned.1.call-update) | async-done | bytes 4718608 | tf_op jit(solution)/shard_map/all_gather | solution.py:31
  390.5 31.1 %all-gather.27.cloned.1.call-done = bf16[4,384,1536]{1,2,0:T(8,128)(2,1)} async-done(((bf16[4,384,192]{1,2,0:T(8,128)(2,1)}), bf16[4,384,1536]{1,2,0:T(8,128)(2,1)}) %all-gather.27.cloned.1.call-update) | async-done | bytes 4718608 | tf_op jit(solution)/shard_map/all_gather | solution.py:35
  437.1 169.4 %all-gather.29.cloned.1.call-done = bf16[4,1536,1536]{2,1,0:T(8,128)(2,1)} async-done(((bf16[4,384,1536]{2,1,0:T(8,128)(2,1)}), bf16[4,1536,1536]{2,1,0:T(8,128)(2,1)}) %all-gather.29.cloned.1.call-update) | async-done | bytes 18874384 | tf_op jit(solution)/shard_map/all_gather | solution.py:28
  624.0 55.1 %reduce-scatter.8.cloned.1.call-done = f32[4,384,192]{1,2,0:T(8,128)} async-done(((f32[4,384,1536]{1,2,0:T(8,128)}), f32[4,384,192]{1,2,0:T(8,128)}) %reduce-scatter.8.cloned.1.call-update) | async-done | bytes 1179664 | tf_op jit(solution)/shard_map/reduce_scatter | solution.py:30
  711.4 34.3 %all-gather.31.cloned.1.call-done = bf16[4,384,1536]{1,2,0:T(8,128)(2,1)} async-done(((bf16[4,384,192]{1,2,0:T(8,128)(2,1)}), bf16[4,384,1536]{1,2,0:T(8,128)(2,1)}) %all-gather.31.cloned.1.call-update) | async-done | bytes 4718608 | tf_op jit(solution)/shard_map/all_gather | solution.py:31
  751.4 31.4 %all-gather.35.cloned.1.call-done = bf16[4,384,1536]{1,2,0:T(8,128)(2,1)} async-done(((bf16[4,384,192]{1,2,0:T(8,128)(2,1)}), bf16[4,384,1536]{1,2,0:T(8,128)(2,1)}) %all-gather.35.cloned.1.call-update) | async-done | bytes 4718608 | tf_op jit(solution)/shard_map/all_gather | solution.py:35
  798.2 169.4 %all-gather.37.cloned.1.call-done = bf16[4,1536,1536]{2,1,0:T(8,128)(2,1)} async-done(((bf16[4,384,1536]{2,1,0:T(8,128)(2,1)}), bf16[4,1536,1536]{2,1,0:T(8,128)(2,1)}) %all-gather.37.cloned.1.call-update) | async-done | bytes 18874384 | tf_op jit(solution)/shard_map/all_gather | solution.py:28
  985.1 55.1 %reduce-scatter.10.cloned.1.call-done = f32[4,384,192]{1,2,0:T(8,128)} async-done(((f32[4,384,1536]{1,2,0:T(8,128)}), f32[4,384,192]{1,2,0:T(8,128)}) %reduce-scatter.10.cloned.1.call-update) | async-done | bytes 1179664 | tf_op jit(solution)/shard_map/reduce_scatter | solution.py:30
  1043.1 29.4 %all-gather.41.cloned.1.call-done = bf16[4,1536,192]{1,2,0:T(8,128)(2,1)} async-done(((bf16[4,384,192]{1,2,0:T(8,128)(2,1)}), bf16[4,1536,192]{1,2,0:T(8,128)(2,1)}) %all-gather.41.cloned.1.call-update) | async-done | bytes 2359312 | tf_op jit(solution)/shard_map/all_gather | solution.py:32
  1072.5 34.2 %all-gather.39.cloned.1.call-done = bf16[4,384,1536]{1,2,0:T(8,128)(2,1)} async-done(((bf16[4,384,192]{1,2,0:T(8,128)(2,1)}), bf16[4,384,1536]{1,2,0:T(8,128)(2,1)}) %all-gather.39.cloned.1.call-update) | async-done | bytes 4718608 | tf_op jit(solution)/shard_map/all_gather | solution.py:31
  1112.4 31.3 %all-gather.43.cloned.1.call-done = bf16[4,384,1536]{1,2,0:T(8,128)(2,1)} async-done(((bf16[4,384,192]{1,2,0:T(8,128)(2,1)}), bf16[4,384,1536]{1,2,0:T(8,128)(2,1)}) %all-gather.43.cloned.1.call-update) | async-done | bytes 4718608 | tf_op jit(solution)/shard_map/all_gather | solution.py:35
  1159.2 169.3 %all-gather.45.cloned.1.call-done = bf16[4,1536,1536]{2,1,0:T(8,128)(2,1)} async-done(((bf16[4,384,1536]{2,1,0:T(8,128)(2,1)}), bf16[4,1536,1536]{2,1,0:T(8,128)(2,1)}) %all-gather.45.cloned.1.call-update) | async-done | bytes 18874384 | tf_op jit(solution)/shard_map/all_gather | solution.py:28
  1346.1 55.1 %reduce-scatter.12.cloned.1.call-done = f32[4,384,192]{1,2,0:T(8,128)} async-done(((f32[4,384,1536]{1,2,0:T(8,128)}), f32[4,384,192]{1,2,0:T(8,128)}) %reduce-scatter.12.cloned.1.call-update) | async-done | bytes 1179664 | tf_op jit(solution)/shard_map/reduce_scatter | solution.py:30
  1433.5 34.3 %all-gather.47.cloned.1.call-done = bf16[4,384,1536]{1,2,0:T(8,128)(2,1)} async-done(((bf16[4,384,192]{1,2,0:T(8,128)(2,1)}), bf16[4,384,1536]{1,2,0:T(8,128)(2,1)}) %all-gather.47.cloned.1.call-update) | async-done | bytes 4718608 | tf_op jit(solution)/shard_map/all_gather | solution.py:31
  1473.6 31.3 %all-gather.51.cloned.1.call-done = bf16[4,384,1536]{1,2,0:T(8,128)(2,1)} async-done(((bf16[4,384,192]{1,2,0:T(8,128)(2,1)}), bf16[4,384,1536]{1,2,0:T(8,128)(2,1)}) %all-gather.51.cloned.1.call-update) | async-done | bytes 4718608 | tf_op jit(solution)/shard_map/all_gather | solution.py:35
  1520.4 169.3 %all-gather.53.cloned.1.call-done = bf16[4,1536,1536]{2,1,0:T(8,128)(2,1)} async-done(((bf16[4,384,1536]{2,1,0:T(8,128)(2,1)}), bf16[4,1536,1536]{2,1,0:T(8,128)(2,1)}) %all-gather.53.cloned.1.call-update) | async-done | bytes 18874384 | tf_op jit(solution)/shard_map/all_gather | solution.py:28
  1707.2 55.1 %reduce-scatter.14.cloned.1.call-done = f32[4,384,192]{1,2,0:T(8,128)} async-done(((f32[4,384,1536]{1,2,0:T(8,128)}), f32[4,384,192]{1,2,0:T(8,128)}) %reduce-scatter.14.cloned.1.call-update) | async-done | bytes 1179664 | tf_op jit(solution)/shard_map/reduce_scatter | solution.py:30
  1765.2 29.4 %all-gather.57.cloned.1.call-done = bf16[4,1536,192]{1,2,0:T(8,128)(2,1)} async-done(((bf16[4,384,192]{1,2,0:T(8,128)(2,1)}), bf16[4,1536,192]{1,2,0:T(8,128)(2,1)}) %all-gather.57.cloned.1.call-update) | async-done | bytes 2359312 | tf_op jit(solution)/shard_map/all_gather | solution.py:32
  1794.7 34.2 %all-gather.55.cloned.1.call-done = bf16[4,384,1536]{1,2,0:T(8,128)(2,1)} async-done(((bf16[4,384,192]{1,2,0:T(8,128)(2,1)}), bf16[4,384,1536]{1,2,0:T(8,128)(2,1)}) %all-gather.55.cloned.1.call-update) | async-done | bytes 4718608 | tf_op jit(solution)/shard_map/all_gather | solution.py:31
  1835.6 30.3 %all-gather.59.cloned.1.call-done = bf16[4,384,1536]{1,2,0:T(8,128)(2,1)} async-done(((bf16[4,384,192]{1,2,0:T(8,128)(2,1)}), bf16[4,384,1536]{1,2,0:T(8,128)(2,1)}) %all-gather.59.cloned.1.call-update) | async-done | bytes 4718608 | tf_op jit(solution)/shard_map/all_gather | solution.py:35
  (75 shorter events, 291.3 us)
Async XLA Ops:
  7.2 238.2 %all-gather.21.cloned.1.call-start = ((), (), s32[]{:S(2)}) async-start(), calls=%async_computation.5 | async-start | bytes 23592960 | tf_op jit(solution)/shard_map/all_gather | solution.py:28
  77.7 240.3 %reduce-scatter.6.cloned.1.call-start = ((), (), s32[]{:S(2)}) async-start(), calls=%async_computation.6 | async-start | bytes 10616832 | tf_op jit(solution)/shard_map/reduce_scatter | solution.py:30
  262.9 87.5 %all-gather.25.cloned.1.call-start = ((), (), s32[]{:S(2)}) async-start(), calls=%async_computation.8 | async-start | bytes 2949120 | tf_op jit(solution)/shard_map/all_gather | solution.py:32
  320.2 64.3 %all-gather.23.cloned.1.call-start = ((), (), s32[]{:S(2)}) async-start(), calls=%async_computation.7 | async-start | bytes 5308416 | tf_op jit(solution)/shard_map/all_gather | solution.py:31
  320.9 100.7 %all-gather.27.cloned.1.call-start = ((), (), s32[]{:S(2)}) async-start(), calls=%async_computation.9 | async-start | bytes 5308416 | tf_op jit(solution)/shard_map/all_gather | solution.py:35
  390.0 216.4 %all-gather.29.cloned.1.call-start = ((), (), s32[]{:S(2)}) async-start(), calls=%async_computation.10 | async-start | bytes 23592960 | tf_op jit(solution)/shard_map/all_gather | solution.py:28
  437.0 242.0 %reduce-scatter.8.cloned.1.call-start = ((), (), s32[]{:S(2)}) async-start(), calls=%async_computation.11 | async-start | bytes 10616832 | tf_op jit(solution)/shard_map/reduce_scatter | solution.py:30
  623.9 87.5 %all-gather.33.cloned.1.call-start = ((), (), s32[]{:S(2)}) async-start(), calls=%async_computation.13 | async-start | bytes 2949120 | tf_op jit(solution)/shard_map/all_gather | solution.py:32
  681.2 64.5 %all-gather.31.cloned.1.call-start = ((), (), s32[]{:S(2)}) async-start(), calls=%async_computation.12 | async-start | bytes 5308416 | tf_op jit(solution)/shard_map/all_gather | solution.py:31
  682.0 100.7 %all-gather.35.cloned.1.call-start = ((), (), s32[]{:S(2)}) async-start(), calls=%async_computation.14 | async-start | bytes 5308416 | tf_op jit(solution)/shard_map/all_gather | solution.py:35
  751.1 216.4 %all-gather.37.cloned.1.call-start = ((), (), s32[]{:S(2)}) async-start(), calls=%async_computation.15 | async-start | bytes 23592960 | tf_op jit(solution)/shard_map/all_gather | solution.py:28
  798.2 242.0 %reduce-scatter.10.cloned.1.call-start = ((), (), s32[]{:S(2)}) async-start(), calls=%async_computation.16 | async-start | bytes 10616832 | tf_op jit(solution)/shard_map/reduce_scatter | solution.py:30
  985.0 87.5 %all-gather.41.cloned.1.call-start = ((), (), s32[]{:S(2)}) async-start(), calls=%async_computation.18 | async-start | bytes 2949120 | tf_op jit(solution)/shard_map/all_gather | solution.py:32
  1043.0 100.7 %all-gather.43.cloned.1.call-start = ((), (), s32[]{:S(2)}) async-start(), calls=%async_computation.19 | async-start | bytes 5308416 | tf_op jit(solution)/shard_map/all_gather | solution.py:35
  1112.2 216.4 %all-gather.45.cloned.1.call-start = ((), (), s32[]{:S(2)}) async-start(), calls=%async_computation.20 | async-start | bytes 23592960 | tf_op jit(solution)/shard_map/all_gather | solution.py:28
  1159.2 242.0 %reduce-scatter.12.cloned.1.call-start = ((), (), s32[]{:S(2)}) async-start(), calls=%async_computation.21 | async-start | bytes 10616832 | tf_op jit(solution)/shard_map/reduce_scatter | solution.py:30
  1346.0 87.5 %all-gather.49.cloned.1.call-start = ((), (), s32[]{:S(2)}) async-start(), calls=%async_computation.23 | async-start | bytes 2949120 | tf_op jit(solution)/shard_map/all_gather | solution.py:32
  1403.4 64.5 %all-gather.47.cloned.1.call-start = ((), (), s32[]{:S(2)}) async-start(), calls=%async_computation.22 | async-start | bytes 5308416 | tf_op jit(solution)/shard_map/all_gather | solution.py:31
  1404.2 100.7 %all-gather.51.cloned.1.call-start = ((), (), s32[]{:S(2)}) async-start(), calls=%async_computation.24 | async-start | bytes 5308416 | tf_op jit(solution)/shard_map/all_gather | solution.py:35
  1473.3 216.4 %all-gather.53.cloned.1.call-start = ((), (), s32[]{:S(2)}) async-start(), calls=%async_computation.25 | async-start | bytes 23592960 | tf_op jit(solution)/shard_map/all_gather | solution.py:28
  1520.3 242.0 %reduce-scatter.14.cloned.1.call-start = ((), (), s32[]{:S(2)}) async-start(), calls=%async_computation.26 | async-start | bytes 10616832 | tf_op jit(solution)/shard_map/reduce_scatter | solution.py:30
  1707.2 87.5 %all-gather.57.cloned.1.call-start = ((), (), s32[]{:S(2)}) async-start(), calls=%async_computation.28 | async-start | bytes 2949120 | tf_op jit(solution)/shard_map/all_gather | solution.py:32
  1764.5 64.3 %all-gather.55.cloned.1.call-start = ((), (), s32[]{:S(2)}) async-start(), calls=%async_computation.27 | async-start | bytes 5308416 | tf_op jit(solution)/shard_map/all_gather | solution.py:31
  1765.1 100.7 %all-gather.59.cloned.1.call-start = ((), (), s32[]{:S(2)}) async-start(), calls=%async_computation.29 | async-start | bytes 5308416 | tf_op jit(solution)/shard_map/all_gather | solution.py:35
  (1 other events, 64.3 us)
Sparse Core Ops, SparseCore 0:
  77.8 167.5 all-gather.20
  263.0 54.9 reduce-scatter.5
  320.3 29.9 all-gather.24
  352.4 32.1 all-gather.22
  390.1 31.4 all-gather.26
  437.1 169.2 all-gather.28
  624.0 54.9 reduce-scatter.7
  681.3 29.9 all-gather.32
  713.6 32.1 all-gather.30
  751.3 31.4 all-gather.34
  798.3 169.2 all-gather.36
  985.2 54.9 reduce-scatter.9
  1074.6 32.1 all-gather.38
  1112.3 31.4 all-gather.42
  1159.3 169.2 all-gather.44
  1346.2 54.9 reduce-scatter.11
  1403.5 29.9 all-gather.48
  1435.7 32.1 all-gather.46
  1473.4 31.4 all-gather.50
  1520.4 169.2 all-gather.52
  1707.3 54.9 reduce-scatter.13
  1764.6 29.9 all-gather.56
  1796.7 32.1 all-gather.54
  1834.4 31.4 all-gather.58
  (1 shorter events, 29.9 us)
where the time goes:
time: 1900 us; the launch traced here: 1890 us
  waiting for transfers between devices  1600 us (84%)
  matrix products  195 us (10%)
  blocking collectives  49.7 us (3%)
  other arithmetic  30.8 us (2%)
    all_gather x5, waiting for transfers between devices, local_step(): x_col = lax.all_gather(x_cur, 'fsdp', axis=1, tiled=True)  845 us
    reduce_scatter x5, waiting for transfers between devices, local_step(): lax.psum_scatter(gram_part, 'tp', scatter_dimension=2, tiled=True)  275 us
    all_gather x5, waiting for transfers between devices, local_step(): gram_row = lax.all_gather(gram_blk, 'tp', axis=2, tiled=True)  171 us
    all_gather x5, waiting for transfers between devices, local_step(): poly_row = lax.all_gather(poly_blk, 'tp', axis=2, tiled=True)  155 us
    all_gather x5, waiting for transfers between devices, local_step(): gram_col = lax.all_gather(gram_blk, 'fsdp', axis=1, tiled=True)  147 us
    dot_general x5, matrix products, local_step(): jnp.einsum('lrk,lsk->lrs', x_cur, x_col, preferred_element_type=jnp.float32)  87 us
    dot_general x5, matrix products, local_step(): jnp.einsum('lrk,lkc->lrc', poly_row, x_col, preferred_element_type=jnp.fl...  81.3 us
    psum x1, blocking collectives, local_step(): lax.psum(jnp.sum(x_init * x_init, axis=(1, 2), keepdims=True), ('fsdp', '...  49.7 us
  transfers between devices with their start and end apart: 25, of which 25 were waited for; matrix products, arithmetic and copies ran while one was open for 0% of the time, Pallas kernels for 0%

commit v1 on v0

v1 whole, which is shorter than its diff:
```python
import math
import jax
import jax.numpy as jnp
from jax import lax
from jax.sharding import PartitionSpec as P

NS_STEPS = 5
COEF_A = 3.4445
COEF_B = -4.7750
COEF_C = 2.0315
EPSILON = 1e-7
F32 = jnp.float32
BF16 = jnp.bfloat16


def solution(mesh):
    block_spec = P('stage', 'fsdp', 'tp')
    scalar_spec = P()

    def muon_step(weight, momentum, gradient, learn_rate, momentum_coef, weight_decay):
        n_cols = weight.shape[2]

        def local_step(w_blk, m_blk, g_blk, rate_val, coef_val, decay_val):
            g_wide = g_blk.astype(F32)
            m_new = coef_val * m_blk + g_wide
            x_init = g_wide + coef_val * m_new
            sq_sum = lax.psum(jnp.sum(x_init * x_init, axis=(1, 2), keepdims=True), ('fsdp', 'tp'))
            x_home = (x_init / (jnp.sqrt(sq_sum) + EPSILON)).astype(BF16)
            x = lax.all_to_all(x_home, 'fsdp', split_axis=0, concat_axis=1, tiled=True)
            for _ in range(NS_STEPS):
                part = jnp.einsum('lrk,lsk->lrs', x, x, preferred_element_type=F32)
                mine = lax.psum_scatter(part, 'tp', scatter_dimension=1, tiled=True).astype(BF16)
                gram = lax.all_gather(mine, 'tp', axis=1, tiled=True)
                sq = jnp.einsum('lrk,lks->lrs', gram, gram, preferred_element_type=F32).astype(BF16)
                poly = (COEF_B * gram.astype(F32) + COEF_C * sq.astype(F32)).astype(BF16)
                px = jnp.einsum('lrk,lkc->lrc', poly, x, preferred_element_type=F32)
                x = (COEF_A * x.astype(F32) + px).astype(BF16)
            x_home = lax.all_to_all(x, 'fsdp', split_axis=1, concat_axis=0, tiled=True)
            step_scale = rate_val * 0.2 * math.sqrt(n_cols)
            keep_scale = 1.0 - rate_val * decay_val
            w_new = keep_scale * w_blk - step_scale * x_home.astype(F32)
            return w_new, m_new

        sharded = jax.shard_map(local_step, mesh=mesh, in_specs=(block_spec, block_spec, block_spec, scalar_spec, scalar_spec, scalar_spec), out_specs=(block_spec, block_spec), check_vma=False)
        return sharded(weight, momentum, gradient, learn_rate, momentum_coef, weight_decay)

    return muon_step
```

time: 1900 us -> 922 us (0.49)
  waiting for transfers between devices: 1600 us -> 482 us
  blocking collectives: 49.7 us -> 106 us
  other arithmetic: 30.8 us -> 84.1 us
  local copies, waits for them, and re-layouts: 0 us -> 31.6 us
    all_gather x20 -> x5, waiting for transfers between devices: 1320 us -> 159 us  [local_step(): gram = lax.all_gather(mine, 'tp', axis=1, tiled=True)]
    all_to_all x0 -> x1, blocking collectives: none -> 56 us  [local_step(): x = lax.all_to_all(x_home, 'fsdp', split_axis=0, concat_axis=1, tiled=True)]
    all_to_all x0 -> x1, waiting for transfers between devices: none -> 52.7 us  [local_step(): x_home = lax.all_to_all(x, 'fsdp', split_axis=1, concat_axis=0, tiled=True)]
    unnamed x0 -> x1, other arithmetic: none -> 31.9 us
    unnamed x0 -> x6, local copies, waits for them, and re-layouts: none -> 22 us
    dot_general x15 -> x10, matrix products: 195 us -> 187 us  [the longest x5 122 us: local_step(): px = jnp.einsum('lrk,lkc->lrc', poly, x, preferred_element_type=F32)]
  transfers between devices with their start and end apart: 25 -> 11, of which waited for: 25 -> 11; matrix products, arithmetic and copies ran while one was open for 0% -> 0% of each run, Pallas kernels for 0% -> 0%
where the time goes in v1:
time: 922 us; the launch traced here: 914 us
  waiting for transfers between devices  482 us (52%)
  matrix products  187 us (20%)
  blocking collectives  106 us (11%)
  other arithmetic  84.1 us (9%)
  local copies, waits for them, and re-layouts  31.6 us (3%)
  between operations  16.7 us (2%)
    reduce_scatter x5, waiting for transfers between devices, local_step(): lax.psum_scatter(part, 'tp', scatter_dimension=1, tiled=True).astype(BF16)  270 us
    all_gather x5, waiting for transfers between devices, local_step(): gram = lax.all_gather(mine, 'tp', axis=1, tiled=True)  159 us
    dot_general x5, matrix products, local_step(): px = jnp.einsum('lrk,lkc->lrc', poly, x, preferred_element_type=F32)  122 us
    dot_general x5, matrix products, local_step(): part = jnp.einsum('lrk,lsk->lrs', x, x, preferred_element_type=F32)  64.2 us
    all_to_all x1, blocking collectives, local_step(): x = lax.all_to_all(x_home, 'fsdp', split_axis=0, concat_axis=1, tiled=True)  56 us
    all_to_all x1, waiting for transfers between devices, local_step(): x_home = lax.all_to_all(x, 'fsdp', split_axis=1, concat_axis=0, tiled=True)  52.7 us
    psum x1, blocking collectives, local_step(): lax.psum(jnp.sum(x_init * x_init, axis=(1, 2), keepdims=True), ('fsdp', '...  49.7 us
    unnamed x1, other arithmetic  31.9 us
  transfers between devices with their start and end apart: 11, of which 11 were waited for; matrix products, arithmetic and copies ran while one was open for 0% of the time, Pallas kernels for 0%

profile of v1, /device:TPU:97, one launch (start us, length us, event | category | flops | bytes accessed | tf_op | source)
XLA Modules:
  0.0 914.5 jit_solution(16860585057250632267)
XLA Ops:
  18.9 49.7 %psum.7 = f32[4,1,1]{0,2,1:T(1,128)S(1)} all-reduce(f32[4,1,1]{0,2,1:T(1,128)S(1)} %bitcast.126), channel_id=1, replica_groups=mesh['stage'=1,'fsdp'=4,'tp'=8] {'fsdp','tp'}, use_global_device_ids=true, to_apply=%region_1.0 | all-reduce | flops 4 | bytes 32 | tf_op jit(solution)/shard_map/psum | solution.py:27
  75.5 56.0 %all_to_all.21 = bf16[4,384,1536]{2,1,0:T(8,128)(2,1)S(1)} all-to-all(bf16[4,384,1536]{2,1,0:T(8,128)(2,1)S(1)} %divide_convert_fusion), channel_id=1, replica_groups=mesh['stage'=1,'fsdp'=4,'tp'=8] {'fsdp'}, dimensions={0} | all-to-all | bytes 9437184 | tf_op jit(solution)/shard_map/all_to_all | solution.py:29
  143.8 53.7 %reduce-scatter.6.cloned.1.call-done = f32[1,192,1536]{2,1,0:T(8,128)} async-done(((f32[1,1536,1536]{2,1,0:T(8,128)}), f32[1,192,1536]{2,1,0:T(8,128)}) %reduce-scatter.6.cloned.1.call-update) | async-done | bytes 1179664 | tf_op jit(solution)/shard_map/reduce_scatter | solution.py:32
  200.2 31.4 %all-gather.6.cloned.1.call-done = bf16[1,1536,1536]{2,1,0:T(8,128)(2,1)} async-done(((bf16[1,192,1536]{2,1,0:T(8,128)(2,1)}), bf16[1,1536,1536]{2,1,0:T(8,128)(2,1)}) %all-gather.6.cloned.1.call-update) | async-done | bytes 4718608 | tf_op jit(solution)/shard_map/all_gather | solution.py:33
  231.7 24.4 %add_convert_fusion.4 = bf16[1536,1536]{1,0:T(8,128)(2,1)} fusion(bf16[1536,1536]{1,0:T(8,128)(2,1)} %bitcast.125, bf16[1,1536,1536]{2,1,0:T(8,128)(2,1)} %all-gather.6.cloned.1.call-done), kind=kOutput, calls=%fused_computation.17 | convolution fusion | flops 14521466880 | bytes 14155776 | tf_op jit(solution)/shard_map/lrk,lkc->lrc/dot_general | solution.py:36
  256.1 13.5 %convolution_bitcast_fusion.3 = f32[1,1536,1536]{2,1,0:T(8,128)} fusion(bf16[1536,1536]{1,0:T(8,128)(2,1)} %add_convert_fusion.4), kind=kOutput, calls=%fused_computation.24 | convolution fusion | flops 7247757312 | bytes 14155776 | tf_op jit(solution)/shard_map/lrk,lsk->lrs/dot_general | solution.py:31
  269.8 54.3 %reduce-scatter.8.cloned.1.call-done = f32[1,192,1536]{2,1,0:T(8,128)} async-done(((f32[1,1536,1536]{2,1,0:T(8,128)}), f32[1,192,1536]{2,1,0:T(8,128)}) %reduce-scatter.8.cloned.1.call-update) | async-done | bytes 1179664 | tf_op jit(solution)/shard_map/reduce_scatter | solution.py:32
  326.5 31.8 %all-gather.8.cloned.1.call-done = bf16[1,1536,1536]{2,1,0:T(8,128)(2,1)} async-done(((bf16[1,192,1536]{2,1,0:T(8,128)(2,1)}), bf16[1,1536,1536]{2,1,0:T(8,128)(2,1)}) %all-gather.8.cloned.1.call-update) | async-done | bytes 4718608 | tf_op jit(solution)/shard_map/all_gather | solution.py:33
  358.3 24.6 %add_convert_fusion.3 = bf16[1536,1536]{1,0:T(8,128)(2,1)} fusion(bf16[1536,1536]{1,0:T(8,128)(2,1)} %add_convert_fusion.4, bf16[1,1536,1536]{2,1,0:T(8,128)(2,1)} %all-gather.8.cloned.1.call-done), kind=kOutput, calls=%fused_computation.16 | convolution fusion | flops 14521466880 | bytes 14155776 | tf_op jit(solution)/shard_map/lrk,lkc->lrc/dot_general | solution.py:36
  382.8 13.6 %convolution_bitcast_fusion.2 = f32[1,1536,1536]{2,1,0:T(8,128)} fusion(bf16[1536,1536]{1,0:T(8,128)(2,1)} %add_convert_fusion.3), kind=kOutput, calls=%fused_computation.23 | convolution fusion | flops 7247757312 | bytes 14155776 | tf_op jit(solution)/shard_map/lrk,lsk->lrs/dot_general | solution.py:31
  396.6 54.2 %reduce-scatter.10.cloned.1.call-done = f32[1,192,1536]{2,1,0:T(8,128)} async-done(((f32[1,1536,1536]{2,1,0:T(8,128)}), f32[1,192,1536]{2,1,0:T(8,128)}) %reduce-scatter.10.cloned.1.call-update) | async-done | bytes 1179664 | tf_op jit(solution)/shard_map/reduce_scatter | solution.py:32
  453.3 31.7 %all-gather.10.cloned.1.call-done = bf16[1,1536,1536]{2,1,0:T(8,128)(2,1)} async-done(((bf16[1,192,1536]{2,1,0:T(8,128)(2,1)}), bf16[1,1536,1536]{2,1,0:T(8,128)(2,1)}) %all-gather.10.cloned.1.call-update) | async-done | bytes 4718608 | tf_op jit(solution)/shard_map/all_gather | solution.py:33
  485.0 24.4 %add_convert_fusion.2 = bf16[1536,1536]{1,0:T(8,128)(2,1)} fusion(bf16[1536,1536]{1,0:T(8,128)(2,1)} %add_convert_fusion.3, bf16[1,1536,1536]{2,1,0:T(8,128)(2,1)} %all-gather.10.cloned.1.call-done), kind=kOutput, calls=%fused_computation.15 | convolution fusion | flops 14521466880 | bytes 14155776 | tf_op jit(solution)/shard_map/lrk,lkc->lrc/dot_general | solution.py:36
  509.5 13.5 %convolution_bitcast_fusion.1 = f32[1,1536,1536]{2,1,0:T(8,128)} fusion(bf16[1536,1536]{1,0:T(8,128)(2,1)} %add_convert_fusion.2), kind=kOutput, calls=%fused_computation.22 | convolution fusion | flops 7247757312 | bytes 14155776 | tf_op jit(solution)/shard_map/lrk,lsk->lrs/dot_general | solution.py:31
  523.2 54.2 %reduce-scatter.12.cloned.1.call-done = f32[1,192,1536]{2,1,0:T(8,128)} async-done(((f32[1,1536,1536]{2,1,0:T(8,128)}), f32[1,192,1536]{2,1,0:T(8,128)}) %reduce-scatter.12.cloned.1.call-update) | async-done | bytes 1179664 | tf_op jit(solution)/shard_map/reduce_scatter | solution.py:32
  579.9 31.7 %all-gather.12.cloned.1.call-done = bf16[1,1536,1536]{2,1,0:T(8,128)(2,1)} async-done(((bf16[1,192,1536]{2,1,0:T(8,128)(2,1)}), bf16[1,1536,1536]{2,1,0:T(8,128)(2,1)}) %all-gather.12.cloned.1.call-update) | async-done | bytes 4718608 | tf_op jit(solution)/shard_map/all_gather | solution.py:33
  611.6 24.6 %add_convert_fusion.1 = bf16[1536,1536]{1,0:T(8,128)(2,1)} fusion(bf16[1536,1536]{1,0:T(8,128)(2,1)} %add_convert_fusion.2, bf16[1,1536,1536]{2,1,0:T(8,128)(2,1)} %all-gather.12.cloned.1.call-done), kind=kOutput, calls=%fused_computation.14 | convolution fusion | flops 14521466880 | bytes 14155776 | tf_op jit(solution)/shard_map/lrk,lkc->lrc/dot_general | solution.py:36
  636.2 13.6 %convolution_bitcast_fusion = f32[1,1536,1536]{2,1,0:T(8,128)} fusion(bf16[1536,1536]{1,0:T(8,128)(2,1)} %add_convert_fusion.1), kind=kOutput, calls=%fused_computation.21 | convolution fusion | flops 7247757312 | bytes 14155776 | tf_op jit(solution)/shard_map/lrk,lsk->lrs/dot_general | solution.py:31
  650.2 54.0 %reduce-scatter.14.cloned.1.call-done = f32[1,192,1536]{2,1,0:T(8,128)} async-done(((f32[1,1536,1536]{2,1,0:T(8,128)}), f32[1,192,1536]{2,1,0:T(8,128)}) %reduce-scatter.14.cloned.1.call-update) | async-done | bytes 1179664 | tf_op jit(solution)/shard_map/reduce_scatter | solution.py:32
  706.4 32.0 %all-gather.14.cloned.1.call-done = bf16[1,1536,1536]{2,1,0:T(8,128)(2,1)} async-done(((bf16[1,192,1536]{2,1,0:T(8,128)(2,1)}), bf16[1,1536,1536]{2,1,0:T(8,128)(2,1)}) %all-gather.14.cloned.1.call-update) | async-done | bytes 4718608 | tf_op jit(solution)/shard_map/all_gather | solution.py:33
  738.4 24.3 %fusion.10 = bf16[1,1536,1536]{2,1,0:T(8,128)(2,1)} fusion(bf16[1536,1536]{1,0:T(8,128)(2,1)} %add_convert_fusion.1, bf16[1,1536,1536]{2,1,0:T(8,128)(2,1)} %all-gather.14.cloned.1.call-done), kind=kOutput, calls=%fused_computation.36 | convolution fusion | flops 14521466880 | bytes 14155776 | tf_op jit(solution)/shard_map/lrk,lkc->lrc/dot_general | solution.py:36
  772.8 31.9 %reduce = bf16[1536,1536]{1,0:T(8,128)(2,1)} reduce(bf16[1536,1,1536]{2,1,0:T(2,128)(2,1)} %bitcast.122, bf16[]{:T(256)} %broadcast.74), dimensions={1}, to_apply=%bitcast.121.reduce_sub_computation | reduce | bytes 9437186
  818.0 52.7 %all-to-all-done.1 = bf16[4,2,294912]{2,1,0:T(2,128)(2,1)} async-done(((bf16[4,2,294912]{2,1,0:T(2,128)(2,1)}), bf16[4,2,294912]{2,1,0:T(2,128)(2,1)}, u32[]{:S(2)}, u32[]{:S(2)}) %all-to-all-start.1) | async-done | bytes 4718624 | tf_op jit(solution)/shard_map/all_to_all | solution.py:38
  894.6 12.5 %multiply_subtract_fusion = f32[4,384,1536]{2,1,0:T(8,128)} fusion(f32[4,384,1536]{2,1,0:T(8,128)} %bitcast.123, f32[4,384,1536]{2,1,0:T(8,128)} %param.6, f32[]{:T(128)S(6)} %sub.6), kind=kLoop, calls=%fused_computation.20 | loop fusion | flops 4718592 | bytes 28311556 | tf_op jit(solution)/shard_map/sub | solution.py:41
  (38 shorter events, 89.3 us)
Async XLA Ops:
  7.2 190.3 %reduce-scatter.6.cloned.1.call-start = ((), (), s32[]{:S(2)}) async-start(), calls=%async_computation.7 | async-start | bytes 10616832 | tf_op jit(solution)/shard_map/reduce_scatter | solution.py:32
  131.5 2.2 copy-start
  143.7 88.0 %all-gather.6.cloned.1.call-start = ((), (), s32[]{:S(2)}) async-start(), calls=%async_computation.8 | async-start | bytes 5308416 | tf_op jit(solution)/shard_map/all_gather | solution.py:33
  199.7 124.4 %reduce-scatter.8.cloned.1.call-start = ((), (), s32[]{:S(2)}) async-start(), calls=%async_computation.9 | async-start | bytes 10616832 | tf_op jit(solution)/shard_map/reduce_scatter | solution.py:32
  269.7 88.6 %all-gather.8.cloned.1.call-start = ((), (), s32[]{:S(2)}) async-start(), calls=%async_computation.10 | async-start | bytes 5308416 | tf_op jit(solution)/shard_map/all_gather | solution.py:33
  326.3 124.5 %reduce-scatter.10.cloned.1.call-start = ((), (), s32[]{:S(2)}) async-start(), calls=%async_computation.11 | async-start | bytes 10616832 | tf_op jit(solution)/shard_map/reduce_scatter | solution.py:32
  396.5 88.6 %all-gather.10.cloned.1.call-start = ((), (), s32[]{:S(2)}) async-start(), calls=%async_computation.12 | async-start | bytes 5308416 | tf_op jit(solution)/shard_map/all_gather | solution.py:33
  453.0 124.4 %reduce-scatter.12.cloned.1.call-start = ((), (), s32[]{:S(2)}) async-start(), calls=%async_computation.13 | async-start | bytes 10616832 | tf_op jit(solution)/shard_map/reduce_scatter | solution.py:32
  523.1 88.5 %all-gather.12.cloned.1.call-start = ((), (), s32[]{:S(2)}) async-start(), calls=%async_computation.14 | async-start | bytes 5308416 | tf_op jit(solution)/shard_map/all_gather | solution.py:33
  579.6 124.6 %reduce-scatter.14.cloned.1.call-start = ((), (), s32[]{:S(2)}) async-start(), calls=%async_computation.15 | async-start | bytes 10616832 | tf_op jit(solution)/shard_map/reduce_scatter | solution.py:32
  649.8 88.6 %all-gather.14.cloned.1.call-start = ((), (), s32[]{:S(2)}) async-start(), calls=%async_computation.16 | async-start | bytes 5308416 | tf_op jit(solution)/shard_map/all_gather | solution.py:33
  811.3 59.4 %all-to-all-start.1 = ((bf16[4,2,294912]{2,1,0:T(2,128)(2,1)}), bf16[4,2,294912]{2,1,0:T(2,128)(2,1)}, u32[]{:S(2)}, u32[]{:S(2)}) async-start(bf16[4,2,294912]{2,1,0:T(2,128)(2,1)} %reshape.139), calls=%async_computation.6 | async-start | bytes 9437184 | tf_op jit(solution)/shard_map/all_to_all | solution.py:38
Sparse Core Ops, SparseCore 0:
  143.8 53.5 reduce-scatter.5
  199.8 31.8 all-gather.5
  269.8 54.1 reduce-scatter.7
  326.4 31.8 all-gather.7
  396.6 54.1 reduce-scatter.9
  453.1 31.8 all-gather.9
  523.2 54.1 reduce-scatter.11
  579.7 31.8 all-gather.11
  650.0 54.1 reduce-scatter.13
  706.5 31.8 all-gather.13

commit v2 on v1

v2 whole, which is shorter than its diff:
```python
import functools
import math

import jax
import jax.numpy as jnp
from jax import lax
from jax.experimental import pallas as pl
from jax.experimental.pallas import tpu as pltpu
from jax.sharding import PartitionSpec as P

NS_STEPS = 5
COEF_A = 3.4445
COEF_B = -4.7750
COEF_C = 2.0315
EPSILON = 1e-7
F32 = jnp.float32
BF16 = jnp.bfloat16
MESH = pl.DeviceIdType.MESH
N_STRIP = 4
N_SUB = 2
NT = (((1,), (1,)), ((), ()))


def muon_kernel(strip, cols, sq_ref, x0_hbm, out_hbm,
                x0, xs, relay_in, relay_out, x, part, pair, ring, packed, gram, poly, nrm_y, nrm_x, nrm_c, nrm,
                x0_sem, own_sem, nrm_s, nrm_r, a2a_s, a2a_r, ret_s, ret_r,
                pair_s, pair_r, rs_s, rs_r, ag_s, ag_r, pg_s, pg_r, poly_s, poly_r):
    f = lax.axis_index('fsdp')
    tp = lax.axis_index('tp')
    chip, core = tp // 2, tp % 2
    sub3 = strip // 3
    half_rows = (2 * sub3 + strip + strip // 2) // 2
    piece = half_rows // N_SUB
    hop = 1 - 2 * core

    def wrap(i):
        return lax.rem(i + 2 * N_STRIP, N_STRIP)

    def y_dev(k):
        return {'fsdp': wrap(f + k)}

    def x_dev(k):
        return {'tp': 2 * wrap(chip + k) + core}

    partner = {'tp': 2 * chip + (1 - core)}
    ahead = x_dev(hop)

    def send(src, dst, s_sem, r_sem, dev):
        copy = pltpu.make_async_remote_copy(src_ref=src, dst_ref=dst, send_sem=s_sem, recv_sem=r_sem,
                                            device_id=dev, device_id_type=MESH)
        copy.start()
        return copy

    loads = [pltpu.make_async_copy(x0_hbm.at[i], x0.at[i], x0_sem.at[i]) for i in range(N_STRIP)]
    for c in loads:
        c.start()

    barrier = pltpu.get_barrier_semaphore()
    for dev in [y_dev(1), y_dev(2), y_dev(3), x_dev(1), x_dev(2), x_dev(3), partner]:
        pl.semaphore_signal(barrier, inc=1, device_id=dev, device_id_type=MESH)
    pl.semaphore_wait(barrier, 7)

    nrm_y[f] = sq_ref[...]
    cs = [send(sq_ref, nrm_y.at[f], nrm_s.at[k - 1], nrm_r.at[k - 1], y_dev(k)) for k in (1, 2, 3)]
    for c in cs:
        c.wait()
    nrm_x[chip] = (nrm_y[0] + nrm_y[1]) + (nrm_y[2] + nrm_y[3])
    cs = [send(nrm_x.at[chip], nrm_x.at[chip], nrm_s.at[k + 2], nrm_r.at[k + 2], x_dev(k)) for k in (1, 2, 3)]
    for c in cs:
        c.wait()
    nrm_c[core] = (nrm_x[0] + nrm_x[1]) + (nrm_x[2] + nrm_x[3])
    send(nrm_c.at[core], nrm_c.at[core], nrm_s.at[6], nrm_r.at[6], partner).wait()
    nrm[...] = 1.0 / (jnp.sqrt(nrm_c[0] + nrm_c[1]) + EPSILON)
    for c in loads:
        c.wait()

    tile = strip // 6
    h = strip // 2

    def scale_to(i, dst, base):
        inv = nrm[pl.ds(i, 1), :][:, 0:1]

        @pl.loop(0, strip // tile)
        def _(r):
            rows = pl.ds(pl.multiple_of(r * tile, tile), tile)
            dst[pl.ds(pl.multiple_of(base + r * tile, tile), tile), :] = (x0[i, rows, :] * inv).astype(BF16)

    def exchange(src, dst, relay, s_sem, r_sem, make):
        make(2)
        r0 = send(src(2).at[pl.ds(0, h)], relay.at[0], s_sem.at[0], r_sem.at[0], y_dev(1))
        r1 = send(src(2).at[pl.ds(h, h)], relay.at[1], s_sem.at[1], r_sem.at[1], y_dev(-1))
        make(1)
        d0 = send(src(1), dst(0), s_sem.at[2], r_sem.at[2], y_dev(1))
        make(-1)
        d1 = send(src(-1), dst(0), s_sem.at[3], r_sem.at[3], y_dev(-1))
        make(0)
        r0.wait_recv()
        f0 = send(relay.at[0], dst(-1).at[pl.ds(0, h)], s_sem.at[4], r_sem.at[4], y_dev(1))
        r1.wait_recv()
        f1 = send(relay.at[1], dst(1).at[pl.ds(h, h)], s_sem.at[5], r_sem.at[5], y_dev(-1))
        r0.wait_send()
        r1.wait_send()
        for c in (d0, d1, f0, f1):
            c.wait()

    def strip_of(ref, i):
        return ref.at[pl.ds(pl.multiple_of(i * strip, strip), strip)]

    def make_in(k):
        i = wrap(f + k)
        if k == 0:
            scale_to(i, x.at[0], i * strip)
        else:
            scale_to(i, xs.at[i], 0)

    exchange(lambda k: xs.at[wrap(f + k)], lambda k: strip_of(x.at[0], wrap(f + k)), relay_in, a2a_s, a2a_r, make_in)
    x[0, pl.ds(N_STRIP * strip, strip), :] = x[0, pl.ds(0, strip), :]

    mine = pl.multiple_of(core * half_rows, 16)
    theirs = pl.multiple_of((1 - core) * half_rows, 16)

    def my_rows(u):
        return pl.ds(pl.multiple_of(core * half_rows + u * piece, 16), piece)

    def gram_strip(cur, q):
        left = x[cur, pl.ds(pl.multiple_of(q * strip, strip), strip), :]
        right = x[cur, pl.ds(pl.multiple_of(q * strip, strip), 2 * strip), :]
        both = lax.dot_general(left, right, NT, preferred_element_type=F32)
        for j in range(3):
            a = slice(j * sub3, (j + 1) * sub3)
            j1 = (j + 1) % 3
            part[q, 0:sub3, a] = both[a, a]
            part[q, sub3:2 * sub3, a] = both[a, j1 * sub3:(j1 + 1) * sub3]
        part[q, pl.ds(2 * sub3, strip), :] = both[:, strip:]
        p, hh = q % 2, q // 2
        left = x[cur, pl.ds(pl.multiple_of(p * strip + hh * h, h), h), :]
        right = x[cur, pl.ds(pl.multiple_of((p + 2) * strip, strip), strip), :]
        part[q, pl.ds(2 * sub3 + strip, h), :] = lax.dot_general(left, right, NT, preferred_element_type=F32)

    def unpack():
        for q in range(N_STRIP):
            r = q * strip
            for j in range(3):
                j1 = (j + 1) % 3
                a = pl.ds(r + j * sub3, sub3)
                b = pl.ds(r + j1 * sub3, sub3)
                gram[a, a] = packed[q, pl.ds(0, sub3), pl.ds(j * sub3, sub3)]
                off = packed[q, pl.ds(sub3, sub3), pl.ds(j * sub3, sub3)]
                gram[a, b] = off
                gram[b, a] = off.T
            n = ((q + 1) % N_STRIP) * strip
            off = packed[q, pl.ds(2 * sub3, strip), :]
            gram[pl.ds(r, strip), pl.ds(n, strip)] = off
            gram[pl.ds(n, strip), pl.ds(r, strip)] = off.T
        for p in range(2):
            top = packed[p, pl.ds(2 * sub3 + strip, h), :]
            low = packed[p + 2, pl.ds(2 * sub3 + strip, h), :]
            off = jnp.concatenate([top, low], axis=0)
            gram[pl.ds(p * strip, strip), pl.ds((p + 2) * strip, strip)] = off
            gram[pl.ds((p + 2) * strip, strip), pl.ds(p * strip, strip)] = off.T

    n_tile = cols // 2
    m_tile = N_STRIP * strip // 2

    @pl.loop(0, NS_STEPS)
    def _(it):
        cur = it % 2
        nxt = 1 - cur

        pairs = {}

        def do_gram(j, off):
            q = wrap(chip + off)
            gram_strip(cur, q)
            pairs[j] = send(part.at[q, pl.ds(theirs, half_rows)], pair.at[q], pair_s.at[j], pair_r.at[j], partner)

        rs = {}

        def rs_send(t):
            q = wrap(chip - hop * (t + 1))
            for u in range(N_SUB):
                rows = my_rows(u)
                val = part[q, rows, :] + pair[q, pl.ds(u * piece, piece), :]
                if t > 0:
                    rs[t - 1, u].wait_recv()
                    val = val + ring[t - 1, pl.ds(u * piece, piece), :]
                part[q, rows, :] = val
                rs[t, u] = send(part.at[q, rows], ring.at[t, pl.ds(u * piece, piece)], rs_s.at[t, u], rs_r.at[t, u], ahead)

        do_gram(0, -1)
        do_gram(1, 1)
        pairs[0].wait_recv()
        pairs[1].wait_recv()
        rs_send(0)
        do_gram(2, 2)
        do_gram(3, 0)
        pairs[2].wait_recv()
        rs_send(1)
        rs_send(2)
        pairs[3].wait_recv()

        ag, pg = {}, {}

        def ag_send(t, u):
            q = wrap(chip - hop * t)
            piece_ref = packed.at[q, my_rows(u)]
            if t < N_STRIP - 1:
                ag[t, u] = send(piece_ref, piece_ref, ag_s.at[t, u], ag_r.at[t, u], ahead)
            pg[t, u] = send(piece_ref, piece_ref, pg_s.at[t, u], pg_r.at[t, u], partner)

        for u in range(N_SUB):
            rows = my_rows(u)
            val = part[chip, rows, :] + pair[chip, pl.ds(u * piece, piece), :]
            rs[2, u].wait_recv()
            packed[chip, rows, :] = (val + ring[2, pl.ds(u * piece, piece), :]).astype(BF16)
            ag_send(0, u)
        for t in range(1, N_STRIP):
            for u in range(N_SUB):
                ag[t - 1, u].wait_recv()
                ag_send(t, u)
        for j in range(4):
            pairs[j].wait_send()
        for c in list(rs.values()) + list(ag.values()):
            c.wait_send()
        for c in pg.values():
            c.wait()
        unpack()

        poly_copies = []
        for k in range(2):
            rows = pl.ds(pl.multiple_of((2 * core + k) * strip, strip), strip)
            lhs = gram[rows, :]
            for n in range(2):
                nc = pl.ds(n * m_tile, m_tile)
                sq = jnp.dot(lhs, gram[:, nc], preferred_element_type=F32).astype(BF16)
                poly[rows, nc] = (COEF_B * gram[rows, nc].astype(F32) + COEF_C * sq.astype(F32)).astype(BF16)
            poly_copies.append(send(poly.at[rows], poly.at[rows], poly_s.at[k], poly_r.at[k], partner))

        def apply_poly(i):
            rows = pl.ds(pl.multiple_of(i * strip, strip), strip)
            lhs = poly[rows, :]
            for n in range(2):
                nc = pl.ds(n * n_tile, n_tile)
                px = jnp.dot(lhs, x[cur, pl.ds(0, N_STRIP * strip), nc], preferred_element_type=F32)
                new = (COEF_A * x[cur, rows, nc].astype(F32) + px).astype(BF16)
                x[nxt, rows, nc] = new

                @pl.when(i == 0)
                def _():
                    x[nxt, pl.ds(N_STRIP * strip, strip), nc] = new

        @pl.loop(0, 2)
        def _(k):
            apply_poly(2 * core + k)

        for c in poly_copies:
            c.wait()

        @pl.loop(0, 2)
        def _(k):
            apply_poly(2 * (1 - core) + k)

    last = NS_STEPS % 2
    own = pltpu.make_async_copy(strip_of(x.at[last], f), out_hbm.at[f], own_sem)

    def make_out(k):
        if k == 0:
            own.start()

    exchange(lambda k: strip_of(x.at[last], wrap(f + k)), lambda k: out_hbm.at[wrap(f + k)], relay_out, ret_s, ret_r, make_out)
    own.wait()


def orthogonalize(sq, x0):
    n_mat, strip, cols = x0.shape
    rows = N_STRIP * strip
    packed_rows = 2 * (strip // 3) + strip + strip // 2
    half_rows = packed_rows // 2
    dma = pltpu.SemaphoreType.DMA
    return pl.pallas_call(
        functools.partial(muon_kernel, strip, cols),
        out_shape=jax.ShapeDtypeStruct((n_mat, strip, cols), BF16),
        in_specs=[pl.BlockSpec(memory_space=pltpu.VMEM), pl.BlockSpec(memory_space=pl.ANY)],
        out_specs=pl.BlockSpec(memory_space=pl.ANY),
        scratch_shapes=[
            pltpu.VMEM((N_STRIP, strip, cols), F32),
            pltpu.VMEM((N_STRIP, strip, cols), BF16),
            pltpu.VMEM((2, strip // 2, cols), BF16),
            pltpu.VMEM((2, strip // 2, cols), BF16),
            pltpu.VMEM((2, rows + strip, cols), BF16),
            pltpu.VMEM((N_STRIP, packed_rows, strip), F32),
            pltpu.VMEM((N_STRIP, half_rows, strip), F32),
            pltpu.VMEM((N_STRIP - 1, half_rows, strip), F32),
            pltpu.VMEM((N_STRIP, packed_rows, strip), BF16),
            pltpu.VMEM((rows, rows), BF16),
            pltpu.VMEM((rows, rows), BF16),
            pltpu.VMEM((N_STRIP,) + sq.shape, F32),
            pltpu.VMEM((N_STRIP,) + sq.shape, F32),
            pltpu.VMEM((2,) + sq.shape, F32),
            pltpu.VMEM(sq.shape, F32),
            dma((N_STRIP,)), dma, dma((7,)), dma((7,)), dma((6,)), dma((6,)), dma((6,)), dma((6,)),
            dma((4,)), dma((4,)), dma((3, N_SUB)), dma((3, N_SUB)), dma((3, N_SUB)), dma((3, N_SUB)),
            dma((4, N_SUB)), dma((4, N_SUB)), dma((2,)), dma((2,)),
        ],
        compiler_params=pltpu.CompilerParams(collective_id=0, has_side_effects=True, vmem_limit_bytes=62 * 1024 * 1024),
        name='muon_ns',
    )(sq, x0)


def solution(mesh):
    block_spec = P('stage', 'fsdp', 'tp')
    scalar_spec = P()
    assert mesh.shape['fsdp'] == N_STRIP and mesh.shape['tp'] == 2 * N_STRIP

    def muon_step(weight, momentum, gradient, learn_rate, momentum_coef, weight_decay):
        n_cols = weight.shape[2]

        def local_step(w_blk, m_blk, g_blk, rate_val, coef_val, decay_val):
            g_wide = g_blk.astype(F32)
            m_new = coef_val * m_blk + g_wide
            x_init = g_wide + coef_val * m_new
            sq = jnp.sum(x_init * x_init, axis=(1, 2))
            sq = jnp.broadcast_to(jnp.concatenate([sq, sq])[:, None], (2 * N_STRIP, 128))
            x_home = orthogonalize(sq, x_init)
            step_scale = rate_val * 0.2 * math.sqrt(n_cols)
            keep_scale = 1.0 - rate_val * decay_val
            w_new = keep_scale * w_blk - step_scale * x_home.astype(F32)
            return w_new, m_new

        sharded = jax.shard_map(local_step, mesh=mesh, in_specs=(block_spec, block_spec, block_spec, scalar_spec, scalar_spec, scalar_spec), out_specs=(block_spec, block_spec), check_vma=False)
        return sharded(weight, momentum, gradient, learn_rate, momentum_coef, weight_decay)

    return muon_step
```

time: 922 us -> 444 us (0.48)
  waiting for transfers between devices: 482 us -> 0 us
  Pallas kernels: 0 us -> 416 us
  matrix products: 187 us -> 0 us
  blocking collectives: 106 us -> 0 us
  other arithmetic: 84.1 us -> 24.6 us
  local copies, waits for them, and re-layouts: 31.6 us -> 0.66 us
  between operations: 16.7 us -> 2.58 us
    pallas_call x0 -> x1, Pallas kernels: none -> 416 us  [orthogonalize(): pl.pallas_call(functools.partial(muon_kernel, strip, cols), out_shape=jax...]
    reduce_scatter x5 -> x0, waiting for transfers between devices: 270 us -> none  [local_step(): lax.psum_scatter(part, 'tp', scatter_dimension=1, tiled=True).astype(BF16)]
    dot_general x10 -> x0, matrix products: 187 us -> none  [the longest x5 122 us: local_step(): px = jnp.einsum('lrk,lkc->lrc', poly, x, preferred_element_type=F32)]
    all_gather x5 -> x0, waiting for transfers between devices: 159 us -> none  [local_step(): gram = lax.all_gather(mine, 'tp', axis=1, tiled=True)]
    all_to_all x1 -> x0, blocking collectives: 56 us -> none  [local_step(): x = lax.all_to_all(x_home, 'fsdp', split_axis=0, concat_axis=1, tiled=True)]
    all_to_all x1 -> x0, waiting for transfers between devices: 52.7 us -> none  [local_step(): x_home = lax.all_to_all(x, 'fsdp', split_axis=1, concat_axis=0, tiled=True)]
    psum x1 -> x0, blocking collectives: 49.7 us -> none  [local_step(): lax.psum(jnp.sum(x_init * x_init, axis=(1, 2), keepdims=True), ('fsdp', '...]
    unnamed x1 -> x0, other arithmetic: 31.9 us -> none
  transfers between devices with their start and end apart: 11 -> 0, of which waited for: 11 -> 0; matrix products, arithmetic and copies ran while one was open for 0% -> 0% of each run, Pallas kernels for 0% -> 0%
where the time goes in v2:
time: 444 us
  Pallas kernels  416 us (94%)
  other arithmetic  24.6 us (6%)
    pallas_call x1, Pallas kernels, orthogonalize(): pl.pallas_call(functools.partial(muon_kernel, strip, cols), out_shape=jax...  416 us
    reduce_sum x1, other arithmetic, local_step(): sq = jnp.sum(x_init * x_init, axis=(1, 2))  13.7 us
    sub x1, other arithmetic, local_step(): w_new = keep_scale * w_blk - step_scale * x_home.astype(F32)  10.9 us

profile of v2, /device:TPU:97, one launch (start us, length us, event | category | flops | bytes accessed | tf_op | source)
XLA Modules:
  0.0 443.6 jit_solution(13654566924491623469)
XLA Ops:
  1.3 13.7 %multiply_reduce_fusion = (f32[4]{0:T(128)S(1)}, f32[4,384,1536]{2,1,0:T(8,128)}, f32[4,384,1536]{2,1,0:T(8,128)}) fusion(f32[]{:T(128)S(6)} %copy.9, bf16[4,384,1536]{2,1,0:T(8,128)(2,1)} %param.8, f32[4,384,1536]{2,1,0:T(8,128)} %param.7), kind=kLoop, calls=%fused_computation.3 | loop fusion | flops 16515068 | bytes 33030164 | tf_op jit(solution)/shard_map/reduce_sum | solution.py:322
  15.0 0.1 pad_maximum_fusion
  15.1 0.7 broadcast_in_dim.2.sq_ref
  15.7 415.7 %muon_ns.1 = bf16[4,384,1536]{2,1,0:T(8,128)(2,1)} custom-call(f32[8,128]{1,0:T(8,128)} %broadcast_in_dim.2.sq_ref, f32[4,384,1536]{2,1,0:T(8,128)} %get-tuple-element.3.x0_hbm), custom_call_target="tpu_custom_call" | custom-call | tf_op jit(solution)/shard_map/muon_ns/pallas_call | solution.py:280
  432.7 10.9 %multiply_subtract_fusion = f32[4,384,1536]{2,1,0:T(8,128)} fusion(bf16[4,384,1536]{2,1,0:T(8,128)(2,1)} %muon_ns.1, f32[4,384,1536]{2,1,0:T(8,128)} %param.6, f32[]{:T(128)S(6)} %mul.35, f32[]{:T(128)S(6)} %sub.6), kind=kLoop, calls=%fused_computation.2 | loop fusion | flops 9437184 | bytes 23592968 | tf_op jit(solution)/shard_map/sub | solution.py:327

commit v3 on v1

v3 whole, which is shorter than its diff:
```python
import functools
import math

import jax
import jax.numpy as jnp
from jax import lax
from jax.experimental import pallas as pl
from jax.experimental.pallas import tpu as pltpu
from jax.sharding import PartitionSpec as P

NS_STEPS = 5
COEF_A = 3.4445
COEF_B = -4.7750
COEF_C = 2.0315
EPSILON = 1e-7
F32 = jnp.float32
BF16 = jnp.bfloat16
MESH = pl.DeviceIdType.MESH
N_STRIP = 4
N_PIECE = 4
NT = (((1,), (1,)), ((), ()))


def piece_lens(strip):
    last = (2 * (strip // 3) + 3 * strip) // (2 * N_STRIP)
    low = last // 32 * 16
    return [(4 * (strip // 3) + strip) // (2 * N_STRIP), (2 * (strip // 3) + 2 * strip) // (2 * N_STRIP), last - low, low]


def muon_kernel(strip, cols, sq_ref, x0_hbm, out_hbm,
                x0, xs, relay_in, relay_out, x, part, pair, ring, packed, gram, poly, nrm_y, nrm_x, nrm_c, nrm,
                x0_sem, own_sem, nrm_s, nrm_r, a2a_s, a2a_r, ret_s, ret_r,
                pair_s, pair_r, s1_s, s1_r, s2_s, s2_r, g1_s, g1_r, g2_s, g2_r, pg_s, pg_r, poly_s, poly_r):
    f = lax.axis_index('fsdp')
    tp = lax.axis_index('tp')
    chip, core = tp // 2, tp % 2
    sub3 = strip // 3

    def wrap(i):
        return lax.rem(i + 2 * N_STRIP, N_STRIP)

    def y_dev(k):
        return {'fsdp': wrap(f + k)}

    def x_dev(k):
        return {'tp': 2 * wrap(chip + k) + core}

    partner = {'tp': 2 * chip + (1 - core)}
    up, down = x_dev(1), x_dev(-1)

    def copy_to(src, dst, s_sem, r_sem, dev):
        return pltpu.make_async_remote_copy(src_ref=src, dst_ref=dst, send_sem=s_sem, recv_sem=r_sem,
                                            device_id=dev, device_id_type=MESH)

    def send(src, dst, s_sem, r_sem, dev):
        copy = copy_to(src, dst, s_sem, r_sem, dev)
        copy.start()
        return copy

    loads = [pltpu.make_async_copy(x0_hbm.at[i], x0.at[i], x0_sem.at[i]) for i in range(N_STRIP)]
    for c in loads:
        c.start()

    barrier = pltpu.get_barrier_semaphore()
    for dev in [y_dev(1), y_dev(2), y_dev(3), x_dev(1), x_dev(2), x_dev(3), partner]:
        pl.semaphore_signal(barrier, inc=1, device_id=dev, device_id_type=MESH)
    pl.semaphore_wait(barrier, 7)

    nrm_y[f] = sq_ref[...]
    cs = [send(sq_ref, nrm_y.at[f], nrm_s.at[k - 1], nrm_r.at[k - 1], y_dev(k)) for k in (1, 2, 3)]
    for c in cs:
        c.wait()
    nrm_x[chip] = (nrm_y[0] + nrm_y[1]) + (nrm_y[2] + nrm_y[3])
    cs = [send(nrm_x.at[chip], nrm_x.at[chip], nrm_s.at[k + 2], nrm_r.at[k + 2], x_dev(k)) for k in (1, 2, 3)]
    for c in cs:
        c.wait()
    nrm_c[core] = (nrm_x[0] + nrm_x[1]) + (nrm_x[2] + nrm_x[3])
    send(nrm_c.at[core], nrm_c.at[core], nrm_s.at[6], nrm_r.at[6], partner).wait()
    nrm[...] = 1.0 / (jnp.sqrt(nrm_c[0] + nrm_c[1]) + EPSILON)
    for c in loads:
        c.wait()

    tile = strip // 6
    h = strip // 2

    def scale_to(i, dst, base):
        inv = nrm[pl.ds(i, 1), :][:, 0:1]

        @pl.loop(0, strip // tile)
        def _(r):
            rows = pl.ds(pl.multiple_of(r * tile, tile), tile)
            dst[pl.ds(pl.multiple_of(base + r * tile, tile), tile), :] = (x0[i, rows, :] * inv).astype(BF16)

    def exchange(src, dst, relay, s_sem, r_sem, make):
        make(2)
        r0 = send(src(2).at[pl.ds(0, h)], relay.at[0], s_sem.at[0], r_sem.at[0], y_dev(1))
        r1 = send(src(2).at[pl.ds(h, h)], relay.at[1], s_sem.at[1], r_sem.at[1], y_dev(-1))
        make(1)
        d0 = send(src(1), dst(0), s_sem.at[2], r_sem.at[2], y_dev(1))
        make(-1)
        d1 = send(src(-1), dst(0), s_sem.at[3], r_sem.at[3], y_dev(-1))
        make(0)
        r0.wait_recv()
        f0 = send(relay.at[0], dst(-1).at[pl.ds(0, h)], s_sem.at[4], r_sem.at[4], y_dev(1))
        r1.wait_recv()
        f1 = send(relay.at[1], dst(1).at[pl.ds(h, h)], s_sem.at[5], r_sem.at[5], y_dev(-1))
        r0.wait_send()
        r1.wait_send()
        for c in (d0, d1, f0, f1):
            c.wait()

    def strip_of(ref, i):
        return ref.at[pl.ds(pl.multiple_of(i * strip, strip), strip)]

    def make_in(k):
        if k == 0:
            scale_to(f, x.at[0], 0)
        else:
            scale_to(wrap(f + k), xs.at[wrap(f + k)], 0)
        return xs.at[wrap(f + k)]

    d0 = send(make_in(1), x.at[0, pl.ds(3 * strip, strip)], a2a_s.at[2], a2a_r.at[2], y_dev(1))
    d1 = send(make_in(-1), x.at[0, pl.ds(strip, strip)], a2a_s.at[3], a2a_r.at[3], y_dev(-1))
    far_x = make_in(2)
    r0 = send(far_x.at[pl.ds(0, h)], relay_in.at[0], a2a_s.at[0], a2a_r.at[0], y_dev(1))
    r1 = send(far_x.at[pl.ds(h, h)], relay_in.at[1], a2a_s.at[1], a2a_r.at[1], y_dev(-1))
    make_in(0)
    f0 = copy_to(relay_in.at[0], x.at[0, pl.ds(2 * strip, h)], a2a_s.at[4], a2a_r.at[4], y_dev(1))
    f1 = copy_to(relay_in.at[1], x.at[0, pl.ds(2 * strip + h, h)], a2a_s.at[5], a2a_r.at[5], y_dev(-1))

    lens = piece_lens(strip)
    bases = [sum(lens[:u]) * 2 * N_STRIP for u in range(N_PIECE)]

    cuts = [(n // 32) * 16 if u == 0 else (n + 16) // 32 * 16 for u, n in enumerate(lens)]
    starts = [sum(lens[:u]) for u in range(N_PIECE)]

    def half_of(u, q, second):
        at0 = bases[u] + (core * N_STRIP + q) * lens[u] + (cuts[u] if second else 0)
        return pl.ds(pl.multiple_of(at0, 16), lens[u] - cuts[u] if second else cuts[u])

    def slot_of(u, second):
        return pl.ds(starts[u] + (cuts[u] if second else 0), lens[u] - cuts[u] if second else cuts[u])

    def rows_of(u, c, q):
        return pl.ds(pl.multiple_of(bases[u] + (c * N_STRIP + q) * lens[u], 16), lens[u])

    def strip_rows(i):
        return pl.ds(pl.multiple_of(i * strip, strip), strip)

    at = {}
    fill = 0
    for blk in [(0, 0), (1, 1), (0, 1), (3, 3), (3, 0), (3, 1), (2, 2), (2, 3), (2, 1), (2, 0)]:
        at[blk] = fill
        fill += 2 * sub3 if blk[0] == blk[1] else strip

    def put(blk, val):
        if blk[0] != blk[1]:
            part[pl.ds(at[blk], strip), :] = val
            return
        for j in range(3):
            a = slice(j * sub3, (j + 1) * sub3)
            j1 = (j + 1) % 3
            part[pl.ds(at[blk], sub3), a] = val[a, a]
            part[pl.ds(at[blk] + sub3, sub3), a] = val[a, j1 * sub3:(j1 + 1) * sub3]

    def gram_blocks(b, i, js):
        left = x[b, pl.ds(i * strip, strip), :]
        right = [x[b, pl.ds(j * strip, strip), :] for j in js]
        right = right[0] if len(js) == 1 else jnp.concatenate(right, axis=0)
        prod = lax.dot_general(left, right, NT, preferred_element_type=F32)
        for n, j in enumerate(js):
            put((i, j), prod[:, n * strip:(n + 1) * strip])

    def unpack(blk):
        i, j = blk
        if i != j:
            off = packed[pl.ds(at[blk], strip), :]
            gram[pl.ds(i * strip, strip), pl.ds(j * strip, strip)] = off
            gram[pl.ds(j * strip, strip), pl.ds(i * strip, strip)] = off.T
            return
        for k in range(3):
            ra = pl.ds(i * strip + k * sub3, sub3)
            rb = pl.ds(i * strip + (k + 1) % 3 * sub3, sub3)
            gram[ra, ra] = packed[pl.ds(at[blk], sub3), pl.ds(k * sub3, sub3)]
            off = packed[pl.ds(at[blk] + sub3, sub3), pl.ds(k * sub3, sub3)]
            gram[ra, rb] = off
            gram[rb, ra] = off.T

    def poly_copy(k, i):
        rows = strip_rows(i)
        return pltpu.make_async_remote_copy(src_ref=poly.at[rows], dst_ref=poly.at[rows], send_sem=poly_s.at[k],
                                            recv_sem=poly_r.at[k], device_id=partner, device_id_type=MESH)

    def make_poly(i):
        rows = strip_rows(i)
        lhs = gram[rows, :]
        m_tile = N_STRIP * strip // 2
        for n in range(2):
            nc = pl.ds(n * m_tile, m_tile)
            sq = jnp.dot(lhs, gram[:, nc], preferred_element_type=F32).astype(BF16)
            poly[rows, nc] = (COEF_B * gram[rows, nc].astype(F32) + COEF_C * sq.astype(F32)).astype(BF16)

    def apply_poly(b, i, tiles=(0, 1)):
        rows = strip_rows(i)
        lhs = poly[rows, :]
        n_tile = cols // 2
        for n in tiles:
            nc = pl.ds(n * n_tile, n_tile)
            px = jnp.dot(lhs, x[b, :, nc], preferred_element_type=F32)
            x[1 - b, rows, nc] = (COEF_A * x[b, rows, nc].astype(F32) + px).astype(BF16)

    @pl.loop(0, NS_STEPS)
    def _(it):
        b = it % 2
        old = 1 - b
        c_up, c_down, c_far = wrap(chip + 1), wrap(chip - 1), wrap(chip + 2)
        pairs, first, second, near, far, pg = {}, {}, {}, {}, {}, {}
        b0 = poly_copy(0, core)
        b1 = poly_copy(1, 3 - core)

        def pair_send(u):
            src = pl.ds(pl.multiple_of(bases[u] + (1 - core) * N_STRIP * lens[u], 16), N_STRIP * lens[u])
            pairs[u] = send(part.at[src], pair.at[src], pair_s.at[u], pair_r.at[u], partner)

        def sum_1(u):
            pairs[u].wait_recv()
            for q in (c_far, c_up, c_down):
                rows = rows_of(u, core, q)
                part[rows, :] = part[rows, :] + pair[rows, :]
            for k, dev in ((0, up), (1, down)):
                first[u, k] = send(part.at[half_of(u, c_far, k)], ring.at[0, slot_of(u, k)], s1_s.at[k, u], s1_r.at[k, u], dev)

        def sum_1b(u):
            second[u, 1] = send(part.at[half_of(u, c_up, 1)], ring.at[1, slot_of(u, 1)], s2_s.at[1, u], s2_r.at[1, u], up)
            second[u, 2] = send(part.at[half_of(u, c_down, 0)], ring.at[2, slot_of(u, 0)], s2_s.at[2, u], s2_r.at[2, u], down)

        def sum_2(u):
            for k, q, dev in ((0, c_up, up), (1, c_down, down)):
                first[u, k].wait_recv()
                rows = half_of(u, q, k)
                part[rows, :] = part[rows, :] + ring[0, slot_of(u, k), :]
                second[u, 3 * k] = send(part.at[rows], ring.at[1 + k, slot_of(u, k)], s2_s.at[3 * k, u], s2_r.at[3 * k, u], dev)

        def gather_1(u):
            rows = rows_of(u, core, chip)
            val = part[rows, :] + pair[rows, :]
            for k in range(4):
                second[u, k].wait_recv()
            slot = pl.ds(starts[u], lens[u])
            packed[rows, :] = (val + (ring[1, slot, :] + ring[2, slot, :])).astype(BF16)
            for k, dev in ((0, up), (1, down)):
                near[u, k] = send(packed.at[rows], packed.at[rows], g1_s.at[k, u], g1_r.at[k, u], dev)
            pg[u, 0] = send(packed.at[rows], packed.at[rows], pg_s.at[0, u], pg_r.at[0, u], partner)

        def gather_2(u):
            for k, q, dev in ((0, c_down, up), (1, c_up, down)):
                near[u, k].wait_recv()
                half = half_of(u, q, k)
                far[u, k] = send(packed.at[half], packed.at[half], g2_s.at[k, u], g2_r.at[k, u], dev)
            for k, q in ((1, c_down), (2, c_up)):
                rows = rows_of(u, core, q)
                pg[u, k] = send(packed.at[rows], packed.at[rows], pg_s.at[k, u], pg_r.at[k, u], partner)

        def gather_3(u):
            far[u, 0].wait_recv()
            far[u, 1].wait_recv()
            rows = rows_of(u, core, c_far)
            pg[u, 3] = send(packed.at[rows], packed.at[rows], pg_s.at[3, u], pg_r.at[3, u], partner)

        def arrived(u):
            for t in range(N_STRIP):
                pg[u, t].wait_recv()

        @pl.when(it > 0)
        def _():
            make_poly(core)
            b0.start()
            make_poly(3 - core)
            b1.start()
            apply_poly(old, core)
            b0.wait_recv()
            apply_poly(old, 1 - core)

        @pl.when(it == 0)
        def _():
            d1.wait_recv()

        gram_blocks(b, 0, [0, 1])
        gram_blocks(b, 1, [1])
        pair_send(0)

        @pl.when(it > 0)
        def _():
            b1.wait_recv()
            apply_poly(old, 3, (0,))

        sum_1(0)
        sum_1b(0)

        @pl.when(it > 0)
        def _():
            apply_poly(old, 3, (1,))

        @pl.when(it == 0)
        def _():
            d0.wait_recv()

        gram_blocks(b, 3, [3, 0, 1])
        pair_send(1)
        sum_2(0)

        @pl.when(it > 0)
        def _():
            apply_poly(old, 2, (0,))

        sum_1(1)
        sum_1b(1)

        @pl.when(it > 0)
        def _():
            apply_poly(old, 2, (1,))
            b0.wait_send()
            b1.wait_send()

        gather_1(0)

        @pl.when(it == 0)
        def _():
            r0.wait_recv()
            f0.start()
            r1.wait_recv()
            f1.start()

        sum_2(1)

        @pl.when(it == 0)
        def _():
            f0.wait_recv()
            f1.wait_recv()

        gram_blocks(b, 2, [2, 3])
        gram_blocks(b, 2, [1, 0])
        pair_send(2)
        pair_send(3)
        gather_2(0)
        sum_1(2)
        sum_1(3)
        sum_1b(2)
        sum_1b(3)
        gather_1(1)
        sum_2(2)
        sum_2(3)
        gather_3(0)
        gather_2(1)
        arrived(0)
        for blk in [(0, 0), (1, 1), (0, 1)]:
            unpack(blk)
        gather_1(2)
        gather_1(3)
        gather_3(1)
        arrived(1)
        for blk in [(3, 3), (3, 0), (3, 1)]:
            unpack(blk)
        gather_2(2)
        gather_2(3)
        gather_3(2)
        gather_3(3)
        arrived(2)
        unpack((2, 2))
        unpack((2, 3))
        arrived(3)
        unpack((2, 1))
        unpack((2, 0))
        for group in (pairs, first, second, near, far, pg):
            for c in group.values():
                c.wait_send()

    for c in (d0, d1, r0, r1, f0, f1):
        c.wait_send()

    last = NS_STEPS % 2
    own = pltpu.make_async_copy(x.at[last, pl.ds(0, strip)], out_hbm.at[f], own_sem)
    b0 = poly_copy(0, 2 - core)
    b1 = poly_copy(1, 3 - 3 * core)
    make_poly(2 - core)
    b0.start()
    make_poly(3 - 3 * core)
    b1.start()
    b0.wait_recv()

    def make_out(k):
        if k == -1:
            b1.wait_recv()
        apply_poly(1 - last, k % N_STRIP)
        if k == 0:
            own.start()

    exchange(lambda k: strip_of(x.at[last], k % N_STRIP), lambda k: out_hbm.at[wrap(f + k)], relay_out, ret_s, ret_r, make_out)
    own.wait()
    b0.wait_send()
    b1.wait_send()


def orthogonalize(sq, x0):
    n_mat, strip, cols = x0.shape
    rows = N_STRIP * strip
    packed_rows = 2 * N_STRIP * sum(piece_lens(strip))
    dma = pltpu.SemaphoreType.DMA
    return pl.pallas_call(
        functools.partial(muon_kernel, strip, cols),
        out_shape=jax.ShapeDtypeStruct((n_mat, strip, cols), BF16),
        in_specs=[pl.BlockSpec(memory_space=pltpu.VMEM), pl.BlockSpec(memory_space=pl.ANY)],
        out_specs=pl.BlockSpec(memory_space=pl.ANY),
        scratch_shapes=[
            pltpu.VMEM((N_STRIP, strip, cols), F32),
            pltpu.VMEM((N_STRIP, strip, cols), BF16),
            pltpu.VMEM((2, strip // 2, cols), BF16),
            pltpu.VMEM((2, strip // 2, cols), BF16),
            pltpu.VMEM((2, rows, cols), BF16),
            pltpu.VMEM((packed_rows, strip), F32),
            pltpu.VMEM((packed_rows, strip), F32),
            pltpu.VMEM((N_STRIP - 1, packed_rows // 8, strip), F32),
            pltpu.VMEM((packed_rows, strip), BF16),
            pltpu.VMEM((rows, rows), BF16),
            pltpu.VMEM((rows, rows), BF16),
            pltpu.VMEM((N_STRIP,) + sq.shape, F32),
            pltpu.VMEM((N_STRIP,) + sq.shape, F32),
            pltpu.VMEM((2,) + sq.shape, F32),
            pltpu.VMEM(sq.shape, F32),
            dma((N_STRIP,)), dma, dma((7,)), dma((7,)), dma((6,)), dma((6,)), dma((6,)), dma((6,)),
            dma((N_PIECE,)), dma((N_PIECE,)), dma((2, N_PIECE)), dma((2, N_PIECE)), dma((4, N_PIECE)), dma((4, N_PIECE)),
            dma((2, N_PIECE)), dma((2, N_PIECE)), dma((2, N_PIECE)), dma((2, N_PIECE)),
            dma((4, N_PIECE)), dma((4, N_PIECE)), dma((2,)), dma((2,)),
        ],
        compiler_params=pltpu.CompilerParams(collective_id=0, has_side_effects=True, vmem_limit_bytes=62 * 1024 * 1024),
        name='muon_ns',
    )(sq, x0)


def solution(mesh):
    block_spec = P('stage', 'fsdp', 'tp')
    scalar_spec = P()
    assert mesh.shape['fsdp'] == N_STRIP and mesh.shape['tp'] == 2 * N_STRIP

    def muon_step(weight, momentum, gradient, learn_rate, momentum_coef, weight_decay):
        n_cols = weight.shape[2]

        def local_step(w_blk, m_blk, g_blk, rate_val, coef_val, decay_val):
            g_wide = g_blk.astype(F32)
            m_new = coef_val * m_blk + g_wide
            x_init = g_wide + coef_val * m_new
            sq = jnp.sum(x_init * x_init, axis=(1, 2))
            sq = jnp.broadcast_to(jnp.concatenate([sq, sq])[:, None], (2 * N_STRIP, 128))
            x_home = orthogonalize(sq, x_init)
            step_scale = rate_val * 0.2 * math.sqrt(n_cols)
            keep_scale = 1.0 - rate_val * decay_val
            w_new = keep_scale * w_blk - step_scale * x_home.astype(F32)
            return w_new, m_new

        sharded = jax.shard_map(local_step, mesh=mesh, in_specs=(block_spec, block_spec, block_spec, scalar_spec, scalar_spec, scalar_spec), out_specs=(block_spec, block_spec), check_vma=False)
        return sharded(weight, momentum, gradient, learn_rate, momentum_coef, weight_decay)

    return muon_step
```

time: 922 us -> 394 us (0.43)
  waiting for transfers between devices: 482 us -> 0 us
  Pallas kernels: 0 us -> 366 us
  matrix products: 187 us -> 0 us
  blocking collectives: 106 us -> 0 us
  other arithmetic: 84.1 us -> 24.6 us
  local copies, waits for them, and re-layouts: 31.6 us -> 0.66 us
  between operations: 16.7 us -> 2.58 us
    pallas_call x0 -> x1, Pallas kernels: none -> 366 us  [orthogonalize(): pl.pallas_call(functools.partial(muon_kernel, strip, cols), out_shape=jax...]
    reduce_scatter x5 -> x0, waiting for transfers between devices: 270 us -> none  [local_step(): lax.psum_scatter(part, 'tp', scatter_dimension=1, tiled=True).astype(BF16)]
    dot_general x10 -> x0, matrix products: 187 us -> none  [the longest x5 122 us: local_step(): px = jnp.einsum('lrk,lkc->lrc', poly, x, preferred_element_type=F32)]
    all_gather x5 -> x0, waiting for transfers between devices: 159 us -> none  [local_step(): gram = lax.all_gather(mine, 'tp', axis=1, tiled=True)]
    all_to_all x1 -> x0, blocking collectives: 56 us -> none  [local_step(): x = lax.all_to_all(x_home, 'fsdp', split_axis=0, concat_axis=1, tiled=True)]
    all_to_all x1 -> x0, waiting for transfers between devices: 52.7 us -> none  [local_step(): x_home = lax.all_to_all(x, 'fsdp', split_axis=1, concat_axis=0, tiled=True)]
    psum x1 -> x0, blocking collectives: 49.7 us -> none  [local_step(): lax.psum(jnp.sum(x_init * x_init, axis=(1, 2), keepdims=True), ('fsdp', '...]
    unnamed x1 -> x0, other arithmetic: 31.9 us -> none
  transfers between devices with their start and end apart: 11 -> 0, of which waited for: 11 -> 0; matrix products, arithmetic and copies ran while one was open for 0% -> 0% of each run, Pallas kernels for 0% -> 0%
where the time goes in v3:
time: 394 us
  Pallas kernels  366 us (93%)
  other arithmetic  24.6 us (6%)
    pallas_call x1, Pallas kernels, orthogonalize(): pl.pallas_call(functools.partial(muon_kernel, strip, cols), out_shape=jax...  366 us
    reduce_sum x1, other arithmetic, local_step(): sq = jnp.sum(x_init * x_init, axis=(1, 2))  13.7 us
    sub x1, other arithmetic, local_step(): w_new = keep_scale * w_blk - step_scale * x_home.astype(F32)  10.9 us

profile of v3, /device:TPU:97, one launch (start us, length us, event | category | flops | bytes accessed | tf_op | source)
XLA Modules:
  0.0 393.6 jit_solution(10176125184457116667)
XLA Ops:
  1.3 13.7 %multiply_reduce_fusion = (f32[4]{0:T(128)S(1)}, f32[4,384,1536]{2,1,0:T(8,128)}, f32[4,384,1536]{2,1,0:T(8,128)}) fusion(f32[]{:T(128)S(6)} %copy.9, bf16[4,384,1536]{2,1,0:T(8,128)(2,1)} %param.8, f32[4,384,1536]{2,1,0:T(8,128)} %param.7), kind=kLoop, calls=%fused_computation.3 | loop fusion | flops 16515068 | bytes 33030164 | tf_op jit(solution)/shard_map/reduce_sum | solution.py:452
  15.0 0.1 pad_maximum_fusion
  15.1 0.7 broadcast_in_dim.2.sq_ref
  15.7 365.7 %muon_ns.1 = bf16[4,384,1536]{2,1,0:T(8,128)(2,1)} custom-call(f32[8,128]{1,0:T(8,128)} %broadcast_in_dim.2.sq_ref, f32[4,384,1536]{2,1,0:T(8,128)} %get-tuple-element.3.x0_hbm), custom_call_target="tpu_custom_call" | custom-call | tf_op jit(solution)/shard_map/muon_ns/pallas_call | solution.py:409
  382.7 10.9 %multiply_subtract_fusion = f32[4,384,1536]{2,1,0:T(8,128)} fusion(bf16[4,384,1536]{2,1,0:T(8,128)(2,1)} %muon_ns.1, f32[4,384,1536]{2,1,0:T(8,128)} %param.6, f32[]{:T(128)S(6)} %mul.35, f32[]{:T(128)S(6)} %sub.6), kind=kLoop, calls=%fused_computation.2 | loop fusion | flops 9437184 | bytes 23592968 | tf_op jit(solution)/shard_map/sub | solution.py:457

commit v4 on v3

--- a/solution.py
+++ b/solution.py
@@ -307,12 +307,12 @@
 
         gram_blocks(b, 3, [3, 0, 1])
         pair_send(1)
+
+        @pl.when(it > 0)
+        def _():
+            apply_poly(old, 2, (0,))
+
         sum_2(0)
-
-        @pl.when(it > 0)
-        def _():
-            apply_poly(old, 2, (0,))
-
         sum_1(1)
         sum_1b(1)
 

time: 394 us -> 393 us (level)
  no operation moved by 1% of the time
where the time goes in v4:
time: 393 us
  Pallas kernels  365 us (93%)
  other arithmetic  24.6 us (6%)
    pallas_call x1, Pallas kernels, orthogonalize(): pl.pallas_call(functools.partial(muon_kernel, strip, cols), out_shape=jax...  365 us
    reduce_sum x1, other arithmetic, local_step(): sq = jnp.sum(x_init * x_init, axis=(1, 2))  13.7 us
    sub x1, other arithmetic, local_step(): w_new = keep_scale * w_blk - step_scale * x_home.astype(F32)  10.9 us

profile of v4, /device:TPU:97, one launch (start us, length us, event | category | flops | bytes accessed | tf_op | source)
XLA Modules:
  0.0 393.0 jit_solution(8944747593099918864)
XLA Ops:
  1.3 13.7 %multiply_reduce_fusion = (f32[4]{0:T(128)S(1)}, f32[4,384,1536]{2,1,0:T(8,128)}, f32[4,384,1536]{2,1,0:T(8,128)}) fusion(f32[]{:T(128)S(6)} %copy.9, bf16[4,384,1536]{2,1,0:T(8,128)(2,1)} %param.8, f32[4,384,1536]{2,1,0:T(8,128)} %param.7), kind=kLoop, calls=%fused_computation.3 | loop fusion | flops 16515068 | bytes 33030164 | tf_op jit(solution)/shard_map/reduce_sum | solution.py:452
  15.0 0.1 pad_maximum_fusion
  15.1 0.7 broadcast_in_dim.2.sq_ref
  15.7 365.1 %muon_ns.1 = bf16[4,384,1536]{2,1,0:T(8,128)(2,1)} custom-call(f32[8,128]{1,0:T(8,128)} %broadcast_in_dim.2.sq_ref, f32[4,384,1536]{2,1,0:T(8,128)} %get-tuple-element.3.x0_hbm), custom_call_target="tpu_custom_call" | custom-call | tf_op jit(solution)/shard_map/muon_ns/pallas_call | solution.py:409
  382.2 10.9 %multiply_subtract_fusion = f32[4,384,1536]{2,1,0:T(8,128)} fusion(bf16[4,384,1536]{2,1,0:T(8,128)(2,1)} %muon_ns.1, f32[4,384,1536]{2,1,0:T(8,128)} %param.6, f32[]{:T(128)S(6)} %mul.35, f32[]{:T(128)S(6)} %sub.6), kind=kLoop, calls=%fused_computation.2 | loop fusion | flops 9437184 | bytes 23592968 | tf_op jit(solution)/shard_map/sub | solution.py:457
